TPU v7x, 32 devices: a whole 2x2x4 slice. The times are simulated.
32 devices in a mesh: lat: 8 (over z, x), lon: 4 (over y, core).
Axes of the slice: x: 2, y: 2, z: 4, core: 2. Of those that a mesh axis runs over, the one named last changes fastest.
Arguments:
- fields: float32 [8, 8, 128, 512], P(None, None, 'lat', 'lon'), may hold values from -6 to 6
- ocean_mask: int32 [128, 4], replicated, may hold values from 0 to 1, as said below
- scale_table: float32 [16], replicated, may hold values from 0.5 to 4
- offset_table: float32 [16], replicated, may hold values from -4 to 4
- scale_index: int32 [8], replicated, may hold values from 0 to 15
- offset_index: int32 [8], replicated, may hold values from 0 to 15
Outputs:
- history: float32 [8, 8, 128, 512], P(None, 'lat', 'lon')
- record_range: float32 [2, 8, 8], P(None, None, 'lat')
Inputs may be any that keep to these rules, and one draw needn't show every extreme that they name: `ocean_mask`: each device's block of 16 rows and 128 longitudes holds at least half of 12 (rounded down, and never fewer than one) and at most 12 ocean strips; some block holds exactly 12.
All inputs are finite; a program needn't handle non-finite values.
Results may differ from a plain program's by a relative error of at most 0.00007.
Values sent between devices are 32-bit elements; how exact they have to be, the bound alone decides.
A program may use at most 64 MiB of HBM per device.

v0:
```python
import jax
import jax.numpy as jnp
from jax import lax
from jax.sharding import PartitionSpec as P

STRIP = 128


def per_device(fields, ocean_mask, scale_table, offset_table, scale_index, offset_index):
    nfield, level_count, lat_rows, lon_cells = fields.shape
    lat_count = lax.axis_size("lat")
    lon_count = lax.axis_size("lon")
    lat_pos = lax.axis_index("lat")
    lon_pos = lax.axis_index("lon")
    strips = lon_cells // STRIP
    slab_blocks = lat_count // lon_count
    table_slots = jnp.arange(scale_table.shape[0])
    scale_pick = scale_index[:, None] == table_slots[None, :]
    offset_pick = offset_index[:, None] == table_slots[None, :]
    scales = jnp.sum(jnp.where(scale_pick, scale_table[None, :], 0.0), axis=1)
    offsets = jnp.sum(jnp.where(offset_pick, offset_table[None, :], 0.0), axis=1)
    own_mask = lax.dynamic_slice(
        ocean_mask, (lat_pos * lat_rows, lon_pos * strips), (lat_rows, strips)
    )
    own_live = jnp.repeat(own_mask, STRIP, axis=1) > 0
    packed = (fields - offsets[:, None, None, None]) * scales[:, None, None, None]
    slab_mask = lax.dynamic_slice(
        ocean_mask,
        (lon_pos * slab_blocks * lat_rows, 0),
        (slab_blocks * lat_rows, lon_count * strips),
    )
    slab_live = jnp.repeat(slab_mask, STRIP, axis=1) > 0
    masked_block = jnp.where(own_live[None, None], packed, 0.0)
    history = lax.all_to_all(
        lax.all_to_all(masked_block, "lat", split_axis=1, concat_axis=2, tiled=True),
        "lon",
        split_axis=2,
        concat_axis=3,
        tiled=True,
    )
    highest = jnp.max(jnp.where(slab_live[None, None], history, -jnp.inf), axis=(2, 3))
    negated = jnp.max(jnp.where(slab_live[None, None], -history, -jnp.inf), axis=(2, 3))
    own_levels = lax.pmax(jnp.stack([highest, negated]), "lon")
    record_range = jnp.stack([own_levels[0], -own_levels[1]])
    return (history, record_range)


def solution(mesh):
    return jax.shard_map(
        per_device,
        mesh=mesh,
        in_specs=(P(None, None, "lat", "lon"), P(), P(), P(), P(), P()),
        out_specs=(P(None, "lat", "lon", None), P(None, None, "lat")),
        check_vma=False,
    )
```

profile of v0, /device:TPU:0, one launch (start us, length us, event | category | flops | bytes accessed | tf_op | source)
XLA Modules:
  0.0 46.4 jit_solution(1260978863947469488)
XLA Ops:
  0.6 0.0 copy-start
  0.6 0.7 %copy-done = s32[128,4]{0,1:T(4,128)S(1)} copy-done((s32[128,4]{0,1:T(4,128)S(1)}, s32[128,4]{0,1:T(4,128)}, u32[]{:S(2)}) %copy-start) | copy-done | bytes 2072
  1.3 0.0 copy-start.1
  1.3 0.0 copy-start.2
  1.3 0.0 copy-start.3
  1.3 0.0 copy-start.4
  1.3 0.1 compare_bitcast_fusion
  1.4 0.6 %copy-done.1 = f32[16]{0:T(128)S(1)} copy-done((f32[16]{0:T(128)S(1)}, f32[16]{0:T(128)}, u32[]{:S(2)}) %copy-start.1) | copy-done | bytes 88
  2.0 0.0 copy-done.2
  2.0 0.0 copy-done.3
  2.0 0.0 copy-done.4
  2.0 0.2 select_reduce_fusion.2
  2.2 1.3 %fusion.1 = f32[8,8,16,128]{3,2,0,1:T(8,128)S(1)} fusion(f32[8,8,16,128]{3,2,1,0:T(8,128)} %param.6, f32[8]{0:T(128)S(1)} %get-tuple-element.14, f32[8]{0:T(128)S(1)} %get-tuple-element.15, pred[16]{0:T(512)(128)(4,1)S(1)} %compare_bitcast_fusion), kind=kLoop, calls=%fused_computation.2 | loop fusion | flops 393216 | bytes 1048656 | tf_op jit(solution)/shard_map/jit(_where)/select_n | solution.py:33
  3.5 21.6 %all_to_all.30 = f32[8,8,16,128]{3,2,0,1:T(8,128)S(1)} all-to-all(f32[8,8,16,128]{3,2,0,1:T(8,128)S(1)} %fusion.1), channel_id=1, replica_groups=mesh['lat'=8,'lon'=4] {'lat'}, dimensions={1} | all-to-all | bytes 1048576 | tf_op jit(solution)/shard_map/all_to_all | solution.py:35
  25.2 1.1 %copy.23 = f32[8,1,128,128]{3,0,1,2:T(8,128)} copy(f32[8,1,128,128]{3,2,0,1:T(8,128)S(1)} %bitcast.12) | data formatting | bytes 1048576 | tf_op jit(solution)/shard_map/all_to_all | solution.py:35
  26.3 3.5 %all-to-all-start.1 = ((f32[8,1,128,128]{3,0,1,2:T(8,128)}), f32[8,1,128,128]{3,0,1,2:T(8,128)S(1)}, u32[]{:S(2)}, u32[]{:S(2)}) async-start(f32[8,1,128,128]{3,0,1,2:T(8,128)} %copy.23), calls=%async_computation.1 | async-start | bytes 1048576 | tf_op jit(solution)/shard_map/all_to_all | solution.py:34
  29.7 0.1 dynamic-slice_compare_fusion
  29.8 8.7 %all-to-all-done.1 = f32[8,1,128,128]{3,0,1,2:T(8,128)S(1)} async-done(((f32[8,1,128,128]{3,0,1,2:T(8,128)}), f32[8,1,128,128]{3,0,1,2:T(8,128)S(1)}, u32[]{:S(2)}, u32[]{:S(2)}) %all-to-all-start.1) | async-done | bytes 524320 | tf_op jit(solution)/shard_map/all_to_all | solution.py:34
  38.5 0.1 copy.24
  38.6 0.3 copy.25
  39.0 0.3 select_reduce_fusion.1
  39.3 0.8 %copy.26 = f32[8,1,32,512]{3,2,1,0:T(8,128)} copy(f32[8,1,32,512]{3,1,2,0:T(1,128)S(1)} %bitcast.11) | data formatting | bytes 1048576
  40.1 5.7 %pmax.7 = f32[2,8,1]{1,2,0:T(1,128)S(1)} all-reduce(f32[2,8,1]{1,2,0:T(1,128)S(1)} %pad_maximum_fusion), channel_id=1, replica_groups=mesh['lat'=8,'lon'=4] {'lon'}, use_global_device_ids=true, to_apply=%region_4.5 | all-reduce | flops 16 | bytes 128 | tf_op jit(solution)/shard_map/pmax | solution.py:43
  45.9 0.6 %pad_maximum_fusion.1 = f32[2,8,1]{1,2,0:T(1,128)} fusion(f32[1,8,1]{1,2,0:T(1,128)S(1)} %get-tuple-element.13, f32[1,8,1]{1,2,0:T(1,128)S(1)} %get-tuple-element.12), kind=kLoop, calls=%fused_computation.12 | loop fusion | flops 16 | bytes 128 | tf_op jit(solution)/shard_map/stack | solution.py:44
  (3 shorter events, 0.1 us)
Async XLA Ops:
  0.6 0.7 %copy-start = (s32[128,4]{0,1:T(4,128)S(1)}, s32[128,4]{0,1:T(4,128)}, u32[]{:S(2)}) copy-start(s32[128,4]{0,1:T(4,128)} %param.7) | copy-start | bytes 6148
  1.3 0.7 %copy-start.1 = (f32[16]{0:T(128)S(1)}, f32[16]{0:T(128)}, u32[]{:S(2)}) copy-start(f32[16]{0:T(128)} %param.8) | copy-start | bytes 196
  1.3 0.7 %copy-start.2 = (s32[8]{0:T(128)S(1)}, s32[8]{0:T(128)}, u32[]{:S(2)}) copy-start(s32[8]{0:T(128)} %param.10) | copy-start | bytes 100
  1.3 0.7 %copy-start.3 = (f32[16]{0:T(128)S(1)}, f32[16]{0:T(128)}, u32[]{:S(2)}) copy-start(f32[16]{0:T(128)} %param.9) | copy-start | bytes 196
  1.3 0.7 %copy-start.4 = (s32[8]{0:T(128)S(1)}, s32[8]{0:T(128)}, u32[]{:S(2)}) copy-start(s32[8]{0:T(128)} %param.11) | copy-start | bytes 100
  26.3 12.3 %all-to-all-start.1 = ((f32[8,1,128,128]{3,0,1,2:T(8,128)}), f32[8,1,128,128]{3,0,1,2:T(8,128)S(1)}, u32[]{:S(2)}, u32[]{:S(2)}) async-start(f32[8,1,128,128]{3,0,1,2:T(8,128)} %copy.23), calls=%async_computation.1 | async-start | bytes 1048576 | tf_op jit(solution)/shard_map/all_to_all | solution.py:34
where the time goes:
time: 46.7 us; the launch traced here: 46.4 us
  blocking collectives  27.3 us (58%)
  waiting for transfers between devices  8.7 us (19%)
  local copies, waits for them, and re-layouts  3.72 us (8%)
  starting transfers between devices  3.47 us (7%)
  other arithmetic  2.49 us (5%)
  between operations  0.7 us (1%)
    all_to_all x1, blocking collectives, per_device(): lax.all_to_all(masked_block, 'lat', split_axis=1, concat_axis=2, tiled=True)  21.6 us
    all_to_all x1, waiting for transfers between devices, per_device(): lax.all_to_all(lax.all_to_all(masked_block, 'lat', split_axis=1, concat_a...  8.7 us
    pmax x1, blocking collectives, per_device(): own_levels = lax.pmax(jnp.stack([highest, negated]), 'lon')  5.74 us
    all_to_all x1, starting transfers between devices, per_device(): lax.all_to_all(lax.all_to_all(masked_block, 'lat', split_axis=1, concat_a...  3.47 us
    unnamed x11, local copies, waits for them, and re-layouts  2.14 us
    select_n x1, other arithmetic, per_device(): masked_block = jnp.where(own_live[None, None], packed, 0.0)  1.26 us
    all_to_all x2, local copies, waits for them, and re-layouts, per_device(): lax.all_to_all(masked_block, 'lat', split_axis=1, concat_axis=2, tiled=True)  1.14 us
  transfers between devices with their start and end apart: 1, of which 1 were waited for; matrix products, arithmetic and copies ran while one was open for 0% of the time, Pallas kernels for 0%

commit v1 on v0

--- a/solution.py
+++ b/solution.py
@@ -31,13 +31,10 @@
     )
     slab_live = jnp.repeat(slab_mask, STRIP, axis=1) > 0
     masked_block = jnp.where(own_live[None, None], packed, 0.0)
-    history = lax.all_to_all(
-        lax.all_to_all(masked_block, "lat", split_axis=1, concat_axis=2, tiled=True),
-        "lon",
-        split_axis=2,
-        concat_axis=3,
-        tiled=True,
-    )
+    block = lax.all_to_all(masked_block, "lat", split_axis=1, concat_axis=2, tiled=True)
+    shards = jnp.split(block, lax.axis_size("lon"), axis=2)
+    received = lax.all_to_all(jnp.stack(shards), "lon", 0, 0)
+    history = jnp.concatenate(received, axis=3)
     highest = jnp.max(jnp.where(slab_live[None, None], history, -jnp.inf), axis=(2, 3))
     negated = jnp.max(jnp.where(slab_live[None, None], -history, -jnp.inf), axis=(2, 3))
     own_levels = lax.pmax(jnp.stack([highest, negated]), "lon")

time: 46.7 us -> 46.4 us (level)
  local copies, waits for them, and re-layouts: 3.72 us -> 2.55 us
  other arithmetic: 2.49 us -> 3.32 us
    all_to_all x2 -> x1, local copies, waits for them, and re-layouts: 1.14 us -> 0.04 us  [per_device(): lax.all_to_all(masked_block, 'lat', split_axis=1, concat_axis=2, tiled=True)]
    another operation x0 -> x1, other arithmetic: none -> 0.83 us  [per_device(): received = lax.all_to_all(jnp.stack(shards), 'lon', 0, 0)]
where the time goes in v1:
time: 46.4 us; the launch traced here: 46.1 us
  blocking collectives  27.4 us (59%)
  waiting for transfers between devices  8.7 us (19%)
  starting transfers between devices  3.47 us (7%)
  other arithmetic  3.32 us (7%)
  local copies, waits for them, and re-layouts  2.55 us (5%)
  between operations  0.7 us (2%)
    all_to_all x1, blocking collectives, per_device(): lax.all_to_all(masked_block, 'lat', split_axis=1, concat_axis=2, tiled=True)  21.6 us
    all_to_all x1, waiting for transfers between devices, per_device(): received = lax.all_to_all(jnp.stack(shards), 'lon', 0, 0)  8.7 us
    pmax x1, blocking collectives, per_device(): own_levels = lax.pmax(jnp.stack([highest, negated]), 'lon')  5.76 us
    all_to_all x1, starting transfers between devices, per_device(): received = lax.all_to_all(jnp.stack(shards), 'lon', 0, 0)  3.47 us
    unnamed x11, local copies, waits for them, and re-layouts  2.14 us
    select_n x1, other arithmetic, per_device(): masked_block = jnp.where(own_live[None, None], packed, 0.0)  1.26 us
  transfers between devices with their start and end apart: 1, of which 1 were waited for; matrix products, arithmetic and copies ran while one was open for 0% of the time, Pallas kernels for 0%

profile of v1, /device:TPU:0, one launch (start us, length us, event | category | flops | bytes accessed | tf_op | source)
XLA Modules:
  0.0 46.1 jit_solution(15658703029161010893)
XLA Ops:
  0.6 0.0 copy-start
  0.6 0.7 %copy-done = s32[128,4]{0,1:T(4,128)S(1)} copy-done((s32[128,4]{0,1:T(4,128)S(1)}, s32[128,4]{0,1:T(4,128)}, u32[]{:S(2)}) %copy-start) | copy-done | bytes 2072
  1.3 0.0 copy-start.1
  1.3 0.0 copy-start.2
  1.3 0.0 copy-start.3
  1.3 0.0 copy-start.4
  1.3 0.1 compare_bitcast_fusion
  1.4 0.6 %copy-done.1 = f32[16]{0:T(128)S(1)} copy-done((f32[16]{0:T(128)S(1)}, f32[16]{0:T(128)}, u32[]{:S(2)}) %copy-start.1) | copy-done | bytes 88
  2.0 0.0 copy-done.2
  2.0 0.0 copy-done.3
  2.0 0.0 copy-done.4
  2.0 0.2 select_reduce_fusion.2
  2.2 1.3 %fusion.1 = f32[8,8,16,128]{3,2,0,1:T(8,128)S(1)} fusion(f32[8,8,16,128]{3,2,1,0:T(8,128)} %param.6, f32[8]{0:T(128)S(1)} %get-tuple-element.14, f32[8]{0:T(128)S(1)} %get-tuple-element.15, pred[16]{0:T(512)(128)(4,1)S(1)} %compare_bitcast_fusion), kind=kLoop, calls=%fused_computation.3 | loop fusion | flops 393216 | bytes 1048656 | tf_op jit(solution)/shard_map/jit(_where)/select_n | solution.py:33
  3.5 21.6 %all_to_all.17 = f32[8,8,16,128]{3,2,0,1:T(8,128)S(1)} all-to-all(f32[8,8,16,128]{3,2,0,1:T(8,128)S(1)} %fusion.1), channel_id=1, replica_groups=mesh['lat'=8,'lon'=4] {'lat'}, dimensions={1} | all-to-all | bytes 1048576 | tf_op jit(solution)/shard_map/all_to_all | solution.py:34
  25.2 0.8 %pad_maximum_fusion = f32[4,8,1,32,128]{4,3,1,2,0:T(8,128)} fusion(f32[1,8,1,32,128]{4,3,1,2,0:T(8,128)S(1)} %get-tuple-element.9, f32[1,8,1,32,128]{4,3,1,2,0:T(8,128)S(1)} %get-tuple-element.10, f32[1,8,1,32,128]{4,3,1,2,0:T(8,128)S(1)} %get-tuple-element.11, f32[1,8,1,32,128]{4,3,1,2,0:T(8,128)S(1)} %get-tuple-element.8), kind=kLoop, calls=%fused_computation | loop fusion | flops 393216 | bytes 1048576 | tf_op jit(solution)/shard_map/stack | solution.py:36
  26.0 3.5 %all-to-all-start.1 = ((f32[4,8,1,32,128]{4,3,1,2,0:T(8,128)}), f32[4,8,1,32,128]{4,3,1,2,0:T(8,128)S(1)}, u32[]{:S(2)}, u32[]{:S(2)}) async-start(f32[4,8,1,32,128]{4,3,1,2,0:T(8,128)} %pad_maximum_fusion), calls=%async_computation.1 | async-start | bytes 1048576 | tf_op jit(solution)/shard_map/all_to_all | solution.py:36
  29.5 0.1 dynamic-slice_compare_fusion
  29.6 8.7 %all-to-all-done.1 = f32[4,8,1,32,128]{4,3,1,2,0:T(8,128)S(1)} async-done(((f32[4,8,1,32,128]{4,3,1,2,0:T(8,128)}), f32[4,8,1,32,128]{4,3,1,2,0:T(8,128)S(1)}, u32[]{:S(2)}, u32[]{:S(2)}) %all-to-all-start.1) | async-done | bytes 524320 | tf_op jit(solution)/shard_map/all_to_all | solution.py:36
  38.3 0.3 select_reduce_fusion.1
  38.6 5.8 %pmax.7 = f32[2,8,1]{1,2,0:T(1,128)S(1)} all-reduce(f32[2,8,1]{1,2,0:T(1,128)S(1)} %pad_maximum_fusion.1), channel_id=1, replica_groups=mesh['lat'=8,'lon'=4] {'lon'}, use_global_device_ids=true, to_apply=%region_4.5 | all-reduce | flops 16 | bytes 128 | tf_op jit(solution)/shard_map/pmax | solution.py:40
  44.3 0.3 copy.19
  44.7 0.8 %copy.20 = f32[8,1,32,512]{3,2,1,0:T(8,128)} copy(f32[8,1,32,512]{3,1,2,0:T(1,128)S(1)} %bitcast.19) | data formatting | bytes 1048576
  45.5 0.6 %pad_maximum_fusion.2 = f32[2,8,1]{1,2,0:T(1,128)} fusion(f32[1,8,1]{1,2,0:T(1,128)S(1)} %get-tuple-element.13, f32[1,8,1]{1,2,0:T(1,128)S(1)} %get-tuple-element.12), kind=kLoop, calls=%fused_computation.17 | loop fusion | flops 16 | bytes 128 | tf_op jit(solution)/shard_map/stack | solution.py:41
  (4 shorter events, 0.1 us)
Async XLA Ops:
  0.6 0.7 %copy-start = (s32[128,4]{0,1:T(4,128)S(1)}, s32[128,4]{0,1:T(4,128)}, u32[]{:S(2)}) copy-start(s32[128,4]{0,1:T(4,128)} %param.7) | copy-start | bytes 6148
  1.3 0.7 %copy-start.1 = (f32[16]{0:T(128)S(1)}, f32[16]{0:T(128)}, u32[]{:S(2)}) copy-start(f32[16]{0:T(128)} %param.8) | copy-start | bytes 196
  1.3 0.7 %copy-start.2 = (s32[8]{0:T(128)S(1)}, s32[8]{0:T(128)}, u32[]{:S(2)}) copy-start(s32[8]{0:T(128)} %param.10) | copy-start | bytes 100
  1.3 0.7 %copy-start.3 = (f32[16]{0:T(128)S(1)}, f32[16]{0:T(128)}, u32[]{:S(2)}) copy-start(f32[16]{0:T(128)} %param.9) | copy-start | bytes 196
  1.3 0.7 %copy-start.4 = (s32[8]{0:T(128)S(1)}, s32[8]{0:T(128)}, u32[]{:S(2)}) copy-start(s32[8]{0:T(128)} %param.11) | copy-start | bytes 100
  26.0 12.3 %all-to-all-start.1 = ((f32[4,8,1,32,128]{4,3,1,2,0:T(8,128)}), f32[4,8,1,32,128]{4,3,1,2,0:T(8,128)S(1)}, u32[]{:S(2)}, u32[]{:S(2)}) async-start(f32[4,8,1,32,128]{4,3,1,2,0:T(8,128)} %pad_maximum_fusion), calls=%async_computation.1 | async-start | bytes 1048576 | tf_op jit(solution)/shard_map/all_to_all | solution.py:36
